TPU v7x, 256 devices: a 2x2x32 block of a 4x8x32 slice. The times are simulated.
256 devices in a mesh: rep: 4 (over y, x), section: 2 (over core), wide: 32 (over z).
Axes of the slice: x: 2, y: 2, z: 32, core: 2. Of those that a mesh axis runs over, the one named last changes fastest.
The devices are a block of a 4x8x32 slice.
Arguments:
- acts: bfloat16 [2, 1024, 8192], P('section', 'rep', 'wide'), parts along dimension 1, may hold values from -100 to 100
- norm_gain: bfloat16 [2, 8192], P('section', 'wide'), may hold values from 0.099609375 to 1.8984375
- w_qkv: bfloat16 [2, 8192, 5120], P('section', None, 'wide'), may hold values from -0.0625 to 0.0625
- w_out: bfloat16 [2, 4096, 8192], P('section', None, 'wide'), may hold values from -0.5 to 0.5
- key_cache: bfloat16 [2, 1024, 384, 512], P('section', ('rep', 'wide')), parts along dimension 1, may hold values from -400 to 400
- value_cache: bfloat16 [2, 1024, 384, 512], P('section', ('rep', 'wide')), parts along dimension 1, may hold values from -6 to 6
- cache_lengths: int32 [2, 1024], P('section', ('rep', 'wide')), parts along dimension 1, may hold values from 2 to 384, as said below
- slot_of: int32 [2, 1024], P('section', 'rep'), parts along dimension 1, may hold values from 0 to 255, each once within a row
Outputs:
- handed: bfloat16 [2, 1024, 8192], P('section', 'rep', 'wide'), parts along dimension 1
There are 4 independent parts, one for each index of `rep`. A program takes and returns all parts, laid end to end along the dimension named above; an argument that names none is the same for every part. Nothing has to cross between parts.
Inputs may be any that keep to these rules, and one draw needn't show every extreme that they name: `cache_lengths`: slot j of a section belongs to owner j // 8; in every section some slot holds exactly 384. `slot_of`: each section's row names every slot once.
All inputs are finite; a program needn't handle non-finite values.
Results may differ from a plain program's by a relative error of at most 0.005.
Values may be sent and summed in bfloat16 or wider, within the bound.
No kernel may reach another device: no remote copies, remote signals or barrier semaphores. Data moves between devices by JAX's collectives and lax.ppermute only.
A program may use at most 64 MiB of HBM per device.

v0:
```python
import math
import jax
import jax.numpy as jnp
from jax import lax
from jax.sharding import PartitionSpec as P

D = 8192
HEADS = 32
KV_HEADS = 4
HDIM = 128
epsilon = 1e-05
rope_base = 500000.0
masked_score = -1e30


def copy_for_each(value, axis):
    count = lax.axis_size(axis)
    return lax.all_to_all(
        jnp.broadcast_to(value[None], (count, *value.shape)), axis, 0, 0, tiled=True
    )


def of_everyone(value, axis):
    return copy_for_each(value, axis).sum(axis=0)


def passed_along(value, axis, steps):
    count = lax.axis_size(axis)
    pairs = [(source, (source + steps) % count) for source in range(count)]
    return lax.ppermute(value, axis, pairs)


def rotate(values, position):
    half_dim = HDIM // 2
    exponent = jnp.arange(half_dim, dtype=jnp.float32) * (2.0 / HDIM)
    frequency = jnp.exp(-math.log(rope_base) * exponent)
    angle = position[..., None] * frequency
    cosine = jnp.cos(angle)
    sine = jnp.sin(angle)
    first_half = values[..., :half_dim]
    second_half = values[..., half_dim:]
    return jnp.concatenate(
        [first_half * cosine - second_half * sine, second_half * cosine + first_half * sine],
        axis=-1,
    )


def attend(joined_rows, key_rows, value_rows, lengths_here):
    row_count = joined_rows.shape[0]
    groups = HEADS // KV_HEADS
    query_width = HEADS * HDIM
    kv_width = KV_HEADS * HDIM
    queries = joined_rows[:, :query_width].reshape(row_count, KV_HEADS, groups, HDIM)
    new_keys = joined_rows[:, query_width : query_width + kv_width].reshape(
        row_count, KV_HEADS, HDIM
    )
    new_values = joined_rows[:, query_width + kv_width :].reshape(row_count, KV_HEADS, HDIM)
    position = lengths_here.astype(jnp.float32)
    queries = rotate(queries.astype(jnp.float32), position[:, None, None]).astype(jnp.bfloat16)
    new_keys = rotate(new_keys.astype(jnp.float32), position[:, None]).astype(jnp.bfloat16)
    score_scale = 1.0 / math.sqrt(HDIM)
    cache_span = key_rows.shape[1]
    cached_keys = key_rows.reshape(row_count, cache_span, KV_HEADS, HDIM)
    cached_values = value_rows.reshape(row_count, cache_span, KV_HEADS, HDIM)
    own_score = (
        jnp.einsum("ngqd,ngd->ngq", queries, new_keys, preferred_element_type=jnp.float32)
        * score_scale
    )
    scores = (
        jnp.einsum("ngqd,nlgd->ngql", queries, cached_keys, preferred_element_type=jnp.float32)
        * score_scale
    )
    live_mask = (jnp.arange(cache_span, dtype=jnp.int32)[None, :] < lengths_here[:, None])[
        :, None, None, :
    ]
    masked = jnp.where(live_mask, scores, masked_score)
    peak = jnp.maximum(jnp.max(masked, axis=-1), own_score)
    weights = jnp.where(live_mask, jnp.exp(masked - peak[..., None]), 0.0)
    sums = jnp.sum(weights, axis=-1)
    weighted = jnp.einsum(
        "ngql,nlgd->ngqd",
        weights.astype(jnp.bfloat16),
        cached_values,
        preferred_element_type=jnp.float32,
    )
    own_weight = jnp.exp(own_score - peak)
    denominator = sums + own_weight
    own_rounded = own_weight.astype(jnp.bfloat16).astype(jnp.float32)
    weighted = weighted + own_rounded[..., None] * new_values.astype(jnp.float32)[:, :, None, :]
    return (weighted / denominator[..., None]).reshape(row_count, query_width).astype(jnp.bfloat16)


def shards(acts, norm_gain, w_qkv, w_out, key_cache, value_cache, cache_lengths, slot_of):
    tokens = acts[0].astype(jnp.float32)
    squares = of_everyone(jnp.sum(tokens * tokens, axis=1), "wide")
    normed = (
        tokens * lax.rsqrt(squares / D + epsilon)[:, None] * norm_gain[0].astype(jnp.float32)
    ).astype(jnp.bfloat16)
    slot_table = slot_of[0]
    request_total = slot_table.shape[0]
    request_at_slot = (
        jnp.zeros((request_total,), jnp.int32)
        .at[slot_table]
        .set(jnp.arange(request_total, dtype=jnp.int32))
    )
    projection = w_qkv[0]
    whole = lax.all_gather(normed, "wide", axis=1, tiled=True)
    columns = jnp.dot(whole, projection, preferred_element_type=jnp.float32).astype(jnp.bfloat16)
    joined_rows = lax.all_to_all(
        columns[request_at_slot], "wide", split_axis=0, concat_axis=1, tiled=True
    )
    attended = attend(joined_rows, key_cache[0], value_cache[0], cache_lengths[0])
    out_weight = w_out[0]
    projected = jnp.dot(
        lax.all_gather(attended, "wide", axis=0, tiled=True),
        out_weight,
        preferred_element_type=jnp.float32,
    )
    updated = (tokens + projected[slot_table]).astype(jnp.bfloat16)
    return passed_along(updated[None], "section", 1)


def solution(mesh):
    placed = (
        P("section", "rep", "wide"),
        P("section", "wide"),
        P("section", None, "wide"),
        P("section", None, "wide"),
        P("section", ("rep", "wide"), None, None),
        P("section", ("rep", "wide"), None, None),
        P("section", ("rep", "wide")),
        P("section", "rep"),
    )
    return jax.shard_map(
        shards, mesh=mesh, in_specs=placed, out_specs=P("section", "rep", "wide"), check_vma=False
    )
```

profile of v0, /device:TPU:37, one launch (start us, length us, event | category | flops | bytes accessed | tf_op | source)
XLA Modules:
  0.0 379.6 jit_solution(14781178704558300775)
XLA Ops:
  6.5 0.0 copy-start
  6.6 1.2 fusion.33
  7.7 0.6 broadcast_in_dim.23
  8.4 33.2 %all-to-all-start = ((f32[32,1,256]{2,1,0:T(1,128)}), f32[32,1,256]{2,1,0:T(1,128)S(1)}, u32[]{:S(2)}, u32[]{:S(2)}) async-start(f32[32,1,256]{2,1,0:T(1,128)} %broadcast_in_dim.23), calls=%async_computation | async-start | bytes 65536 | tf_op jit(solution)/shard_map/all_to_all | solution.py:18
  41.6 0.1 all-gather.3.cloned.1.call-start
  41.6 0.7 mul.188
  42.3 20.6 %all-to-all-done = f32[32,1,256]{2,1,0:T(1,128)S(1)} async-done(((f32[32,1,256]{2,1,0:T(1,128)}), f32[32,1,256]{2,1,0:T(1,128)S(1)}, u32[]{:S(2)}, u32[]{:S(2)}) %all-to-all-start) | async-done | bytes 32800 | tf_op jit(solution)/shard_map/all_to_all | solution.py:18
  63.0 0.1 reduce_sum.28
  63.0 1.7 fusion.35
  64.7 0.1 all-gather.3.cloned.1.call-update
  64.8 5.5 %reshape_squeeze.6 = bf16[8,384,4,128]{3,2,1,0:T(4,128)(2,1)} reshape(bf16[1,8,384,512]{3,2,1,0:T(8,128)(2,1)} %param.12) | data formatting | bytes 6291456 | tf_op jit(solution)/shard_map/reshape;squeeze | solution.py:63
  70.3 0.0 copy-start.3
  70.3 5.5 %reshape_squeeze.7 = bf16[8,384,4,128]{3,2,1,0:T(4,128)(2,1)} reshape(bf16[1,8,384,512]{3,2,1,0:T(8,128)(2,1)} %param.13) | data formatting | bytes 6291456 | tf_op jit(solution)/shard_map/reshape;squeeze | solution.py:64
  75.8 0.0 copy-done.3
  75.8 1.4 scatter_custom_fusion
  77.3 0.0 copy-start.4
  77.3 100.0 %all-gather.3.cloned.1.call-done = bf16[256,8192]{1,0:T(8,128)(2,1)} async-done(((bf16[256,256]{1,0:T(8,128)(2,1)}), bf16[256,8192]{1,0:T(8,128)(2,1)}) %all-gather.3.cloned.1.call-update) | async-done | bytes 4194320 | tf_op jit(solution)/shard_map/all_gather | solution.py:107
  177.3 0.0 copy-done
  177.3 3.7 fusion.20
  181.0 0.1 copy.25
  181.1 1.8 gather_fusion
  183.0 12.1 %all-to-all-start.1 = ((bf16[32,8,160]{2,1,0:T(8,128)(2,1)}), bf16[32,8,160]{2,1,0:T(8,128)(2,1)S(1)}, u32[]{:S(2)}, u32[]{:S(2)}) async-start(bf16[32,8,160]{2,1,0:T(8,128)(2,1)} %bitcast.6), calls=%async_computation.1 | async-start | bytes 262144 | tf_op jit(solution)/shard_map/all_to_all | solution.py:109
  195.1 0.1 all-gather.5.cloned.1.call-start
  195.1 0.0 copy-done.4
  195.2 0.1 iota_compare_fusion
  195.2 0.1 multiply_cosine_fusion
  195.3 25.2 %all-to-all-done.1 = bf16[32,8,160]{2,1,0:T(8,128)(2,1)S(1)} async-done(((bf16[32,8,160]{2,1,0:T(8,128)(2,1)}), bf16[32,8,160]{2,1,0:T(8,128)(2,1)S(1)}, u32[]{:S(2)}, u32[]{:S(2)}) %all-to-all-start.1) | async-done | bytes 81952 | tf_op jit(solution)/shard_map/all_to_all | solution.py:109
  220.5 0.2 all_to_all.22
  220.7 0.0 copy-start.1
  220.8 0.1 subtract_convert_fusion.1
  220.9 0.1 subtract_convert_fusion
  221.0 0.1 maximum_bitcast_fusion
  221.1 0.2 fusion.41
  221.3 3.5 fusion.51
  224.8 0.2 fusion.31
  225.1 0.0 copy-done.1
  225.1 0.7 fusion.26
  225.9 0.7 copy.58
  226.5 0.1 all-gather.5.cloned.1.call-update
  226.6 0.0 copy-start.2
  226.6 118.5 %all-gather.5.cloned.1.call-done = bf16[256,4096]{1,0:T(8,128)(2,1)} async-done(((bf16[8,4096]{1,0:T(8,128)(2,1)}), bf16[256,4096]{1,0:T(8,128)(2,1)}) %all-gather.5.cloned.1.call-update) | async-done | bytes 2097168 | tf_op jit(solution)/shard_map/all_gather | solution.py:115
  345.1 2.9 fusion.6
  348.0 1.0 gather_fusion.1
  349.0 0.0 copy-done.2
  349.0 22.1 %collective-permute-start = (bf16[1,256,256]{2,1,0:T(8,128)(2,1)S(1)}, bf16[1,256,256]{2,1,0:T(8,128)(2,1)S(1)}, u32[]{:S(2)}, u32[]{:S(2)}) collective-permute-start(bf16[1,256,256]{2,1,0:T(8,128)(2,1)S(1)} %fusion.36), channel_id=1, source_target_pairs={{0,32},{32,0},{1,33},{33,1},{2,34},{34,2},{3,35},{35,3},{4,36},{36... | collective-permute-start | bytes 393224 | tf_op jit(solution)/shard_map/ppermute | solution.py:30
  371.1 1.0 collective-permute-done
  372.1 0.7 copy.60
  (16 shorter events, 0.2 us)
Async XLA Ops:
  6.5 170.8 %copy-start = (bf16[1,8192,160]{1,2,0:T(8,128)(2,1)S(1)}, bf16[1,8192,160]{1,2,0:T(8,128)(2,1)}, u32[]{:S(2)}) copy-start(bf16[1,8192,160]{1,2,0:T(8,128)(2,1)} %param.10) | copy-start | bytes 7864324
  8.4 54.6 %all-to-all-start = ((f32[32,1,256]{2,1,0:T(1,128)}), f32[32,1,256]{2,1,0:T(1,128)S(1)}, u32[]{:S(2)}, u32[]{:S(2)}) async-start(f32[32,1,256]{2,1,0:T(1,128)} %broadcast_in_dim.23), calls=%async_computation | async-start | bytes 65536 | tf_op jit(solution)/shard_map/all_to_all | solution.py:18
  41.6 135.7 %all-gather.3.cloned.1.call-start = ((), (), s32[]{:S(2)}) async-start(), calls=%async_computation.2 | async-start | bytes 4325376 | tf_op jit(solution)/shard_map/all_gather | solution.py:107
  70.3 5.6 %copy-start.3 = (s32[1,256]{1,0:T(1,128)S(1)}, s32[1,256]{1,0:T(1,128)}, u32[]{:S(2)}) copy-start(s32[1,256]{1,0:T(1,128)} %param.15) | copy-start | bytes 3076
  77.3 117.9 %copy-start.4 = (s32[1,8]{1,0:T(1,128)S(1)}, s32[1,8]{1,0:T(1,128)}, u32[]{:S(2)}) copy-start(s32[1,8]{1,0:T(1,128)} %param.14) | copy-start | bytes 100
  183.0 37.6 %all-to-all-start.1 = ((bf16[32,8,160]{2,1,0:T(8,128)(2,1)}), bf16[32,8,160]{2,1,0:T(8,128)(2,1)S(1)}, u32[]{:S(2)}, u32[]{:S(2)}) async-start(bf16[32,8,160]{2,1,0:T(8,128)(2,1)} %bitcast.6), calls=%async_computation.1 | async-start | bytes 262144 | tf_op jit(solution)/shard_map/all_to_all | solution.py:109
  195.1 150.0 %all-gather.5.cloned.1.call-start = ((), (), s32[]{:S(2)}) async-start(), calls=%async_computation.3 | async-start | bytes 2162688 | tf_op jit(solution)/shard_map/all_gather | solution.py:115
  220.7 4.4 %copy-start.1 = (bf16[8,384,4,128]{3,2,1,0:T(4,128)(2,1)S(1)}, bf16[8,384,4,128]{3,2,1,0:T(4,128)(2,1)}, u32[]{:S(2)}) copy-start(bf16[8,384,4,128]{3,2,1,0:T(4,128)(2,1)} %reshape_squeeze.7) | copy-start | bytes 9437188
  226.6 122.4 %copy-start.2 = (bf16[1,256,256]{2,1,0:T(8,128)(2,1)S(1)}, bf16[1,256,256]{2,1,0:T(8,128)(2,1)}, u32[]{:S(2)}) copy-start(bf16[1,256,256]{2,1,0:T(8,128)(2,1)} %param.8) | copy-start | bytes 393220
  349.0 23.1 %collective-permute-start = (bf16[1,256,256]{2,1,0:T(8,128)(2,1)S(1)}, bf16[1,256,256]{2,1,0:T(8,128)(2,1)S(1)}, u32[]{:S(2)}, u32[]{:S(2)}) collective-permute-start(bf16[1,256,256]{2,1,0:T(8,128)(2,1)S(1)} %fusion.36), channel_id=1, source_target_pairs={{0,32},{32,0},{1,33},{33,1},{2,34},{34,2},{3,35},{35,3},{4,36},{36... | collective-permute-start | bytes 393224 | tf_op jit(solution)/shard_map/ppermute | solution.py:30
Sparse Core Ops, SparseCore 0:
  64.9 112.3 all-gather.2
  226.7 118.3 all-gather.4
where the time goes:
time: 380 us
  waiting for transfers between devices  265 us (70%)
  starting transfers between devices  67.5 us (18%)
  local copies, waits for them, and re-layouts  17.6 us (5%)
  between operations  13.7 us (4%)
  matrix products  11.1 us (3%)
  other arithmetic  4.37 us (1%)
    all_gather x1, waiting for transfers between devices, shards(): lax.all_gather(attended, 'wide', axis=0, tiled=True)  118 us
    all_gather x1, waiting for transfers between devices, shards(): whole = lax.all_gather(normed, 'wide', axis=1, tiled=True)  100 us
    all_to_all x1, starting transfers between devices, copy_for_each(): lax.all_to_all(jnp.broadcast_to(value[None], (count, *value.shape)), axis...  33.2 us
    all_to_all x1, waiting for transfers between devices, shards(): lax.all_to_all(columns[request_at_slot], 'wide', split_axis=0, concat_axi...  25.2 us
    ppermute x1, starting transfers between devices, passed_along(): return lax.ppermute(value, axis, pairs)  22.1 us
    all_to_all x1, waiting for transfers between devices, copy_for_each(): lax.all_to_all(jnp.broadcast_to(value[None], (count, *value.shape)), axis...  20.6 us
    all_to_all x1, starting transfers between devices, shards(): lax.all_to_all(columns[request_at_slot], 'wide', split_axis=0, concat_axi...  12.1 us
  transfers between devices with their start and end apart: 5, of which 5 were waited for; matrix products, arithmetic and copies ran while one was open for 4% of the time, Pallas kernels for 0%

commit v1 on v0

--- a/solution.py
+++ b/solution.py
@@ -112,7 +112,9 @@
     attended = attend(joined_rows, key_cache[0], value_cache[0], cache_lengths[0])
     out_weight = w_out[0]
     projected = jnp.dot(
-        lax.all_gather(attended, "wide", axis=0, tiled=True),
+        jnp.concatenate(
+            lax.all_to_all(jnp.stack([attended] * lax.axis_size("wide")), "wide", 0, 0), axis=0
+        ),
         out_weight,
         preferred_element_type=jnp.float32,
     )

time: 380 us -> 447 us (1.18)
  waiting for transfers between devices: 265 us -> 328 us
    all_to_all x0 -> x1, waiting for transfers between devices: none -> 181 us  [shards(): lax.all_to_all(jnp.stack([attended] * lax.axis_size('wide')), 'wide', 0, 0)]
    all_gather x1 -> x0, waiting for transfers between devices: 118 us -> none  [shards(): lax.all_gather(attended, 'wide', axis=0, tiled=True)]
    all_to_all x0 -> x1, starting transfers between devices: none -> 5.56 us  [shards(): lax.all_to_all(jnp.stack([attended] * lax.axis_size('wide')), 'wide', 0, 0)]
  transfers between devices with their start and end apart: 5 -> 5, of which waited for: 5 -> 5; matrix products, arithmetic and copies ran while one was open for 4% -> 3% of each run, Pallas kernels for 0% -> 0%
where the time goes in v1:
time: 447 us; the launch traced here: 446 us
  waiting for transfers between devices  328 us (73%)
  starting transfers between devices  70 us (16%)
  local copies, waits for them, and re-layouts  18.5 us (4%)
  between operations  13.7 us (3%)
  matrix products  11.1 us (2%)
    all_to_all x1, waiting for transfers between devices, shards(): lax.all_to_all(jnp.stack([attended] * lax.axis_size('wide')), 'wide', 0, 0)  181 us
    all_gather x1, waiting for transfers between devices, shards(): whole = lax.all_gather(normed, 'wide', axis=1, tiled=True)  100 us
    all_to_all x1, starting transfers between devices, copy_for_each(): lax.all_to_all(jnp.broadcast_to(value[None], (count, *value.shape)), axis...  33.2 us
    all_to_all x1, waiting for transfers between devices, shards(): lax.all_to_all(columns[request_at_slot], 'wide', split_axis=0, concat_axi...  25.2 us
    all_to_all x1, waiting for transfers between devices, copy_for_each(): lax.all_to_all(jnp.broadcast_to(value[None], (count, *value.shape)), axis...  20.6 us
    ppermute x1, starting transfers between devices, passed_along(): return lax.ppermute(value, axis, pairs)  19.1 us
    all_to_all x1, starting transfers between devices, shards(): lax.all_to_all(columns[request_at_slot], 'wide', split_axis=0, concat_axi...  12.1 us
  transfers between devices with their start and end apart: 5, of which 5 were waited for; matrix products, arithmetic and copies ran while one was open for 3% of the time, Pallas kernels for 0%

profile of v1, /device:TPU:37, one launch (start us, length us, event | category | flops | bytes accessed | tf_op | source)
XLA Modules:
  0.0 445.9 jit_solution(12549103719042522118)
XLA Ops:
  6.5 0.0 copy-start
  6.6 1.2 fusion.34
  7.7 0.6 broadcast_in_dim.23
  8.4 33.2 %all-to-all-start = ((f32[32,1,256]{2,1,0:T(1,128)}), f32[32,1,256]{2,1,0:T(1,128)S(1)}, u32[]{:S(2)}, u32[]{:S(2)}) async-start(f32[32,1,256]{2,1,0:T(1,128)} %broadcast_in_dim.23), calls=%async_computation | async-start | bytes 65536 | tf_op jit(solution)/shard_map/all_to_all | solution.py:18
  41.6 0.1 all-gather.2.cloned.1.call-start
  41.6 0.7 mul.188
  42.3 20.6 %all-to-all-done = f32[32,1,256]{2,1,0:T(1,128)S(1)} async-done(((f32[32,1,256]{2,1,0:T(1,128)}), f32[32,1,256]{2,1,0:T(1,128)S(1)}, u32[]{:S(2)}, u32[]{:S(2)}) %all-to-all-start) | async-done | bytes 32800 | tf_op jit(solution)/shard_map/all_to_all | solution.py:18
  63.0 0.1 reduce_sum.28
  63.0 1.7 fusion.36
  64.7 0.1 all-gather.2.cloned.1.call-update
  64.8 5.5 %reshape_squeeze.6 = bf16[8,384,4,128]{3,2,1,0:T(4,128)(2,1)} reshape(bf16[1,8,384,512]{3,2,1,0:T(8,128)(2,1)} %param.12) | data formatting | bytes 6291456 | tf_op jit(solution)/shard_map/reshape;squeeze | solution.py:63
  70.3 0.0 copy-start.3
  70.3 5.5 %reshape_squeeze.7 = bf16[8,384,4,128]{3,2,1,0:T(4,128)(2,1)} reshape(bf16[1,8,384,512]{3,2,1,0:T(8,128)(2,1)} %param.13) | data formatting | bytes 6291456 | tf_op jit(solution)/shard_map/reshape;squeeze | solution.py:64
  75.8 0.0 copy-done.3
  75.8 1.4 scatter_custom_fusion
  77.3 0.0 copy-start.4
  77.3 100.0 %all-gather.2.cloned.1.call-done = bf16[256,8192]{1,0:T(8,128)(2,1)} async-done(((bf16[256,256]{1,0:T(8,128)(2,1)}), bf16[256,8192]{1,0:T(8,128)(2,1)}) %all-gather.2.cloned.1.call-update) | async-done | bytes 4194320 | tf_op jit(solution)/shard_map/all_gather | solution.py:107
  177.3 0.0 copy-done
  177.3 3.7 fusion.21
  181.0 0.1 copy.25
  181.1 1.8 gather_fusion
  183.0 12.1 %all-to-all-start.1 = ((bf16[32,8,160]{2,1,0:T(8,128)(2,1)}), bf16[32,8,160]{2,1,0:T(8,128)(2,1)S(1)}, u32[]{:S(2)}, u32[]{:S(2)}) async-start(bf16[32,8,160]{2,1,0:T(8,128)(2,1)} %bitcast.6), calls=%async_computation.1 | async-start | bytes 262144 | tf_op jit(solution)/shard_map/all_to_all | solution.py:109
  195.1 0.0 copy-done.4
  195.1 0.1 iota_compare_fusion
  195.2 0.1 multiply_cosine_fusion
  195.3 25.2 %all-to-all-done.1 = bf16[32,8,160]{2,1,0:T(8,128)(2,1)S(1)} async-done(((bf16[32,8,160]{2,1,0:T(8,128)(2,1)}), bf16[32,8,160]{2,1,0:T(8,128)(2,1)S(1)}, u32[]{:S(2)}, u32[]{:S(2)}) %all-to-all-start.1) | async-done | bytes 81952 | tf_op jit(solution)/shard_map/all_to_all | solution.py:109
  220.5 0.2 all_to_all.25
  220.7 0.0 copy-start.1
  220.8 0.1 subtract_convert_fusion.1
  220.9 0.1 subtract_convert_fusion
  221.0 0.1 maximum_bitcast_fusion
  221.1 0.2 fusion.42
  221.3 3.5 fusion.52
  224.8 0.2 fusion.32
  225.1 0.0 copy-done.1
  225.1 0.7 fusion.27
  225.9 1.5 stack.2
  227.5 5.6 %all-to-all-start.2 = ((bf16[32,8,4096]{2,1,0:T(8,128)(2,1)}), bf16[32,8,4096]{2,1,0:T(8,128)(2,1)}, u32[]{:S(2)}, u32[]{:S(2)}) async-start(bf16[32,8,4096]{2,1,0:T(8,128)(2,1)} %stack.2), calls=%async_computation.2 | async-start | bytes 4194304 | tf_op jit(solution)/shard_map/all_to_all | solution.py:116
  233.0 0.0 copy-start.2
  233.1 181.4 %all-to-all-done.2 = bf16[32,8,4096]{2,1,0:T(8,128)(2,1)} async-done(((bf16[32,8,4096]{2,1,0:T(8,128)(2,1)}), bf16[32,8,4096]{2,1,0:T(8,128)(2,1)}, u32[]{:S(2)}, u32[]{:S(2)}) %all-to-all-start.2) | async-done | bytes 2097184 | tf_op jit(solution)/shard_map/all_to_all | solution.py:116
  414.4 2.9 fusion.6
  417.3 1.0 gather_fusion.1
  418.3 0.0 copy-done.2
  418.4 19.1 %collective-permute-start = (bf16[1,256,256]{2,1,0:T(8,128)(2,1)S(1)}, bf16[1,256,256]{2,1,0:T(8,128)(2,1)S(1)}, u32[]{:S(2)}, u32[]{:S(2)}) collective-permute-start(bf16[1,256,256]{2,1,0:T(8,128)(2,1)S(1)} %fusion.37), channel_id=1, source_target_pairs={{0,32},{32,0},{1,33},{33,1},{2,34},{34,2},{3,35},{35,3},{4,36},{36... | collective-permute-start | bytes 393224 | tf_op jit(solution)/shard_map/ppermute | solution.py:30
  437.4 1.0 collective-permute-done
  438.4 0.7 copy.60
  (17 shorter events, 0.2 us)
Async XLA Ops:
  6.5 170.8 %copy-start = (bf16[1,8192,160]{1,2,0:T(8,128)(2,1)S(1)}, bf16[1,8192,160]{1,2,0:T(8,128)(2,1)}, u32[]{:S(2)}) copy-start(bf16[1,8192,160]{1,2,0:T(8,128)(2,1)} %param.10) | copy-start | bytes 7864324
  8.4 54.6 %all-to-all-start = ((f32[32,1,256]{2,1,0:T(1,128)}), f32[32,1,256]{2,1,0:T(1,128)S(1)}, u32[]{:S(2)}, u32[]{:S(2)}) async-start(f32[32,1,256]{2,1,0:T(1,128)} %broadcast_in_dim.23), calls=%async_computation | async-start | bytes 65536 | tf_op jit(solution)/shard_map/all_to_all | solution.py:18
  41.6 135.7 %all-gather.2.cloned.1.call-start = ((), (), s32[]{:S(2)}) async-start(), calls=%async_computation.3 | async-start | bytes 4325376 | tf_op jit(solution)/shard_map/all_gather | solution.py:107
  70.3 5.5 %copy-start.3 = (s32[1,256]{1,0:T(1,128)S(1)}, s32[1,256]{1,0:T(1,128)}, u32[]{:S(2)}) copy-start(s32[1,256]{1,0:T(1,128)} %param.15) | copy-start | bytes 3076
  77.3 117.8 %copy-start.4 = (s32[1,8]{1,0:T(1,128)S(1)}, s32[1,8]{1,0:T(1,128)}, u32[]{:S(2)}) copy-start(s32[1,8]{1,0:T(1,128)} %param.14) | copy-start | bytes 100
  183.0 37.6 %all-to-all-start.1 = ((bf16[32,8,160]{2,1,0:T(8,128)(2,1)}), bf16[32,8,160]{2,1,0:T(8,128)(2,1)S(1)}, u32[]{:S(2)}, u32[]{:S(2)}) async-start(bf16[32,8,160]{2,1,0:T(8,128)(2,1)} %bitcast.6), calls=%async_computation.1 | async-start | bytes 262144 | tf_op jit(solution)/shard_map/all_to_all | solution.py:109
  220.7 4.4 copy-start.1
  227.5 187.0 %all-to-all-start.2 = ((bf16[32,8,4096]{2,1,0:T(8,128)(2,1)}), bf16[32,8,4096]{2,1,0:T(8,128)(2,1)}, u32[]{:S(2)}, u32[]{:S(2)}) async-start(bf16[32,8,4096]{2,1,0:T(8,128)(2,1)} %stack.2), calls=%async_computation.2 | async-start | bytes 4194304 | tf_op jit(solution)/shard_map/all_to_all | solution.py:116
  233.0 185.3 %copy-start.2 = (bf16[1,256,256]{2,1,0:T(8,128)(2,1)S(1)}, bf16[1,256,256]{2,1,0:T(8,128)(2,1)}, u32[]{:S(2)}) copy-start(bf16[1,256,256]{2,1,0:T(8,128)(2,1)} %param.8) | copy-start | bytes 393220
  418.4 20.1 %collective-permute-start = (bf16[1,256,256]{2,1,0:T(8,128)(2,1)S(1)}, bf16[1,256,256]{2,1,0:T(8,128)(2,1)S(1)}, u32[]{:S(2)}, u32[]{:S(2)}) collective-permute-start(bf16[1,256,256]{2,1,0:T(8,128)(2,1)S(1)} %fusion.37), channel_id=1, source_target_pairs={{0,32},{32,0},{1,33},{33,1},{2,34},{34,2},{3,35},{35,3},{4,36},{36... | collective-permute-start | bytes 393224 | tf_op jit(solution)/shard_map/ppermute | solution.py:30
Sparse Core Ops, SparseCore 0:
  64.9 112.3 all-gather.1
